TPU v7x, 32 devices: a whole 2x2x4 slice. The times are simulated.
32 devices in a mesh: rows: 8 (over z, core), aux: 4 (over y, x).
Axes of the slice: x: 2, y: 2, z: 4, core: 2. Of those that a mesh axis runs over, the one named last changes fastest.
Arguments:
- pair_coeffs: float32 [36000, 8192], P('aux', 'rows'), may hold values from -0.0625 to 0.0625
- pair_gaps: float32 [8192], P('rows'), may hold values from 0.2 to 20
- trial_vectors: float32 [36000, 128], P('aux'), may hold values from -0.03125 to 0.03125
Outputs:
- vectors_out: float32 [36000, 128], P('aux')
- rayleigh: float32 [128, 128], replicated
All inputs are finite; a program needn't handle non-finite values.
Results may differ from a plain program's by a relative error of at most 0.00011.
Values sent between devices are 32-bit elements; how exact they have to be, the bound alone decides.
A program may use at most 128 MiB of HBM per device.

v0:
```python
import jax
import jax.numpy as jnp
from jax import lax
from jax.sharding import PartitionSpec as P

ITERS = 2


def project(coeffs, vectors_now):
    return lax.dot_general(
        coeffs,
        vectors_now,
        (((0,), (0,)), ((), ())),
        precision=lax.Precision.HIGHEST,
        preferred_element_type=jnp.float32,
    )


def shards(pair_coeffs, pair_gaps, trial_vectors):
    highest = lax.Precision.HIGHEST
    weights = 4.0 * pair_gaps / (pair_gaps * pair_gaps + 1.0)

    def forward(vectors_now):
        projected = lax.psum(project(pair_coeffs, vectors_now), "aux")
        return (projected, weights)

    vectors_now = trial_vectors
    for step in range(ITERS):
        apply_projected, apply_row_weights = forward(vectors_now)
        scaled = apply_row_weights[:, None] * apply_projected
        partial_sum = jnp.dot(
            pair_coeffs, scaled, precision=highest, preferred_element_type=jnp.float32
        )
        applied = lax.psum(partial_sum, "rows")
        local_gram = jnp.dot(
            applied.T, applied, precision=highest, preferred_element_type=jnp.float32
        )
        correlation = lax.psum(local_gram, "aux")
        factor = jnp.linalg.cholesky(correlation)
        vectors_now = jax.scipy.linalg.solve_triangular(factor, applied.T, lower=True).T
    final_proj, row_weights = forward(vectors_now)
    local_rayleigh = jnp.dot(
        final_proj.T,
        row_weights[:, None] * final_proj,
        precision=highest,
        preferred_element_type=jnp.float32,
    )
    rayleigh = lax.psum(local_rayleigh, "rows")
    return (vectors_now, rayleigh)


def solution(mesh):
    in_specs = (P("aux", "rows"), P("rows"), P("aux", None))
    out_specs = (P("aux", None), P())
    return jax.shard_map(shards, mesh=mesh, in_specs=in_specs, out_specs=out_specs, check_vma=False)
```

profile of v0, /device:TPU:0, one launch (start us, length us, event | category | flops | bytes accessed | tf_op | source)
XLA Modules:
  0.0 741.6 jit_solution(11998312503589431034)
XLA Ops:
  7.2 27.7 %fusion.19 = f32[1024,128]{0,1:T(8,128)} fusion(f32[9000,1024]{1,0:T(8,128)} %param.6, f32[9000,128]{1,0:T(8,128)} %param.8), kind=kOutput, calls=%fused_computation.33 | convolution fusion | flops 14155776000 | bytes 41996288 | tf_op jit(solution)/shard_map/dot_general | solution.py:10
  35.0 48.2 %all-reduce.9.cloned.1.call-done = f32[1024,128]{0,1:T(8,128)} async-done(((f32[1024,128]{0,1:T(8,128)}), f32[1024,128]{0,1:T(8,128)}) %all-reduce.9.cloned.1.call-update) | async-done | bytes 524304 | tf_op jit(solution)/shard_map/psum | solution.py:24
  83.2 33.3 %convolution_bitcast_fusion.1 = f32[9000,128]{1,0:T(8,128)} fusion(f32[9000,1024]{1,0:T(8,128)} %param.6, f32[1024,128]{0,1:T(8,128)} %all-reduce.9.cloned.1.call-done, f32[1024]{0:T(1024)S(1)} %add_divide_fusion), kind=kOutput, calls=%fused_computation.1 | convolution fusion | flops 14155907072 | bytes 42000384 | tf_op jit(solution)/shard_map/dot_general | solution.py:31
  116.8 104.8 %all-reduce.11.cloned.1.call-done = f32[9000,128]{1,0:T(8,128)} async-done(((f32[9000,128]{1,0:T(8,128)}), f32[9000,128]{1,0:T(8,128)}) %all-reduce.11.cloned.1.call-update) | async-done | bytes 4608016 | tf_op jit(solution)/shard_map/psum | solution.py:34
  221.5 11.8 %fusion.20 = f32[128,128]{0,1:T(8,128)} fusion(f32[9000,128]{1,0:T(8,128)} %all-reduce.11.cloned.1.call-done), kind=kOutput, calls=%fused_computation.34 | convolution fusion | flops 1769472000 | bytes 4673536 | tf_op jit(solution)/shard_map/dot_general | solution.py:35
  233.8 41.4 %all-reduce.13.cloned.1.call-done = f32[128,128]{0,1:T(8,128)} async-done(((f32[128,128]{0,1:T(8,128)}), f32[128,128]{0,1:T(8,128)}) %all-reduce.13.cloned.1.call-update) | async-done | bytes 65552 | tf_op jit(solution)/shard_map/psum | solution.py:38
  276.9 11.7 %cholesky.44 = f32[128,128]{1,0:T(8,128)S(1)} custom-call(f32[128,128]{1,0:T(8,128)S(1)} %fusion.16), custom_call_target="Cholesky" | custom-call | tf_op jit(solution)/shard_map/jit(cholesky)/cholesky | solution.py:39
  290.0 9.8 %custom-call.6 = f32[1,128,128]{1,2,0:T(8,128)S(1)} custom-call(f32[1,128,128]{2,1,0:T(8,128)S(1)} %fusion.11), custom_call_target="InvertDiagBlocksLowerTriangular" | custom-call | tf_op jit(solution)/shard_map/jit(_solve_triangular)/triangular_solve | solution.py:40
  299.8 6.1 fusion.2
  305.9 24.9 %convolution_bitcast_fusion.2 = f32[1024,128]{0,1:T(8,128)} fusion(f32[128,9000]{1,0:T(8,128)S(1)} %fusion.2, f32[9000,1024]{1,0:T(8,128)} %param.6), kind=kOutput, calls=%fused_computation.6 | convolution fusion | flops 14155776000 | bytes 41996288 | tf_op jit(solution)/shard_map/dot_general | solution.py:10
  331.1 45.3 %all-reduce.15.cloned.1.call-done = f32[1024,128]{0,1:T(8,128)} async-done(((f32[1024,128]{0,1:T(8,128)}), f32[1024,128]{0,1:T(8,128)}) %all-reduce.15.cloned.1.call-update) | async-done | bytes 524304 | tf_op jit(solution)/shard_map/psum | solution.py:24
  376.4 33.3 %convolution_bitcast_fusion = f32[9000,128]{1,0:T(8,128)} fusion(f32[9000,1024]{1,0:T(8,128)} %param.6, f32[1024,128]{0,1:T(8,128)} %all-reduce.15.cloned.1.call-done, f32[1024]{0:T(1024)S(1)} %add_divide_fusion), kind=kOutput, calls=%fused_computation | convolution fusion | flops 14155907072 | bytes 42000384 | tf_op jit(solution)/shard_map/dot_general | solution.py:31
  409.7 105.0 %all-reduce.17.cloned.1.call-done = f32[9000,128]{1,0:T(8,128)} async-done(((f32[9000,128]{1,0:T(8,128)}), f32[9000,128]{1,0:T(8,128)}) %all-reduce.17.cloned.1.call-update) | async-done | bytes 4608016 | tf_op jit(solution)/shard_map/psum | solution.py:34
  514.7 11.8 %fusion.21 = f32[128,128]{0,1:T(8,128)} fusion(f32[9000,128]{1,0:T(8,128)} %all-reduce.17.cloned.1.call-done), kind=kOutput, calls=%fused_computation.35 | convolution fusion | flops 1769472000 | bytes 4673536 | tf_op jit(solution)/shard_map/dot_general | solution.py:35
  526.7 41.5 %all-reduce.19.cloned.1.call-done = f32[128,128]{0,1:T(8,128)} async-done(((f32[128,128]{0,1:T(8,128)}), f32[128,128]{0,1:T(8,128)}) %all-reduce.19.cloned.1.call-update) | async-done | bytes 65552 | tf_op jit(solution)/shard_map/psum | solution.py:38
  570.1 11.7 %cholesky.55 = f32[128,128]{1,0:T(8,128)S(1)} custom-call(f32[128,128]{1,0:T(8,128)S(1)} %fusion.14), custom_call_target="Cholesky" | custom-call | tf_op jit(solution)/shard_map/jit(cholesky)/cholesky | solution.py:39
  583.1 9.8 %custom-call.7 = f32[1,128,128]{1,2,0:T(8,128)S(1)} custom-call(f32[1,128,128]{2,1,0:T(8,128)S(1)} %fusion.12), custom_call_target="InvertDiagBlocksLowerTriangular" | custom-call | tf_op jit(solution)/shard_map/jit(_solve_triangular)/triangular_solve | solution.py:40
  593.0 9.2 %fusion = f32[128,9000]{0,1:T(8,128)S(1)} fusion(f32[9000,128]{1,0:T(8,128)} %all-reduce.17.cloned.1.call-done, f32[1,128,128]{1,2,0:T(8,128)S(1)} %custom-call.7), kind=kOutput, calls=%fused_computation.2 | convolution fusion | flops 1769472000 | bytes 9281536 | tf_op jit(solution)/shard_map/jit(_solve_triangular)/triangular_solve | solution.py:40
  602.2 2.1 copy-done
  604.3 25.4 %convolution_bitcast_fusion.3 = f32[1024,128]{0,1:T(8,128)} fusion(f32[128,9000]{0,1:T(8,128)S(1)} %fusion, f32[9000,1024]{1,0:T(8,128)} %param.6), kind=kOutput, calls=%fused_computation.7 | convolution fusion | flops 14155776000 | bytes 41996288 | tf_op jit(solution)/shard_map/dot_general | solution.py:10
  629.8 45.5 %all-reduce.21.cloned.1.call-done = f32[1024,128]{0,1:T(8,128)} async-done(((f32[1024,128]{0,1:T(8,128)}), f32[1024,128]{0,1:T(8,128)}) %all-reduce.21.cloned.1.call-update) | async-done | bytes 524304 | tf_op jit(solution)/shard_map/psum | solution.py:24
  675.3 2.4 fusion.4
  677.7 55.2 %all-reduce.23.cloned.1.call-done = f32[128,128]{1,0:T(8,128)} async-done(((f32[128,128]{1,0:T(8,128)}), f32[128,128]{1,0:T(8,128)}) %all-reduce.23.cloned.1.call-update) | async-done | bytes 65552 | tf_op jit(solution)/shard_map/psum | solution.py:48
  732.9 1.5 copy.19
  (30 shorter events, 7.7 us)
Async XLA Ops:
  7.2 27.8 %copy-start.1 = (f32[1024]{0:T(1024)S(1)}, f32[1024]{0:T(1024)}, u32[]{:S(2)}) copy-start(f32[1024]{0:T(1024)} %param.7) | copy-start | bytes 12292
  7.2 76.0 %all-reduce.9.cloned.1.call-start = ((), (), s32[]{:S(2)}) async-start(), calls=%async_computation | async-start | bytes 1048576 | tf_op jit(solution)/shard_map/psum | solution.py:24
  34.9 186.6 %all-reduce.11.cloned.1.call-start = ((), (), s32[]{:S(2)}) async-start(), calls=%async_computation.1 | async-start | bytes 9216000 | tf_op jit(solution)/shard_map/psum | solution.py:34
  116.5 158.6 %all-reduce.13.cloned.1.call-start = ((), (), s32[]{:S(2)}) async-start(), calls=%async_computation.2 | async-start | bytes 131072 | tf_op jit(solution)/shard_map/psum | solution.py:38
  233.3 143.0 %all-reduce.15.cloned.1.call-start = ((), (), s32[]{:S(2)}) async-start(), calls=%async_computation.3 | async-start | bytes 1048576 | tf_op jit(solution)/shard_map/psum | solution.py:24
  330.8 183.9 %all-reduce.17.cloned.1.call-start = ((), (), s32[]{:S(2)}) async-start(), calls=%async_computation.4 | async-start | bytes 9216000 | tf_op jit(solution)/shard_map/psum | solution.py:34
  409.7 158.6 %all-reduce.19.cloned.1.call-start = ((), (), s32[]{:S(2)}) async-start(), calls=%async_computation.5 | async-start | bytes 131072 | tf_op jit(solution)/shard_map/psum | solution.py:38
  526.5 148.8 %all-reduce.21.cloned.1.call-start = ((), (), s32[]{:S(2)}) async-start(), calls=%async_computation.6 | async-start | bytes 1048576 | tf_op jit(solution)/shard_map/psum | solution.py:24
  602.2 2.2 copy-start
  629.8 103.1 %all-reduce.23.cloned.1.call-start = ((), (), s32[]{:S(2)}) async-start(), calls=%async_computation.7 | async-start | bytes 131072 | tf_op jit(solution)/shard_map/psum | solution.py:48
Sparse Core Ops, SparseCore 0:
  35.1 48.0 all-reduce.8
  116.6 104.8 all-reduce.10
  233.5 41.6 all-reduce.12
  331.0 45.3 all-reduce.14
  409.8 104.8 all-reduce.16
  526.6 41.6 all-reduce.18
  629.9 45.3 all-reduce.20
  678.2 54.6 all-reduce.22
where the time goes:
time: 748 us; the launch traced here: 742 us
  waiting for transfers between devices  487 us (65%)
  matrix products  186 us (25%)
  other arithmetic  47.4 us (6%)
  between operations  14.6 us (2%)
    psum x2, waiting for transfers between devices, shards(): applied = lax.psum(partial_sum, 'rows')  210 us
    psum x3, waiting for transfers between devices, forward(): projected = lax.psum(project(pair_coeffs, vectors_now), 'aux')  139 us
    psum x2, waiting for transfers between devices, shards(): correlation = lax.psum(local_gram, 'aux')  82.9 us
    dot_general x3, matrix products, project(): lax.dot_general(coeffs, vectors_now, (((0,), (0,)), ((), ())), precision=...  78 us
    dot_general x2, matrix products, shards(): jnp.dot(pair_coeffs, scaled, precision=highest, preferred_element_type=jn...  66.6 us
    psum x1, waiting for transfers between devices, shards(): rayleigh = lax.psum(local_rayleigh, 'rows')  55.2 us
    another operation x6, other arithmetic, shards(): factor = jnp.linalg.cholesky(correlation)  24.8 us
    dot_general x2, matrix products, shards(): jnp.dot(applied.T, applied, precision=highest, preferred_element_type=jnp...  23.5 us
  transfers between devices with their start and end apart: 8, of which 8 were waited for; matrix products, arithmetic and copies ran while one was open for 0% of the time, Pallas kernels for 0%

commit v1 on v0

--- a/solution.py
+++ b/solution.py
@@ -21,7 +21,9 @@
     weights = 4.0 * pair_gaps / (pair_gaps * pair_gaps + 1.0)
 
     def forward(vectors_now):
-        projected = lax.psum(project(pair_coeffs, vectors_now), "aux")
+        x = project(pair_coeffs, vectors_now)
+        parts = lax.all_gather(x, "aux")
+        projected = jnp.sum(parts, axis=0)
         return (projected, weights)
 
     vectors_now = trial_vectors

time: 748 us -> 785 us (1.049)
  matrix products: 186 us -> 239 us
  waiting for transfers between devices: 487 us -> 456 us
    psum x3 -> x0, waiting for transfers between devices: 139 us -> none  [forward(): projected = lax.psum(project(pair_coeffs, vectors_now), 'aux')]
    all_gather x0 -> x3, waiting for transfers between devices: none -> 109 us  [forward(): parts = lax.all_gather(x, 'aux')]
    dot_general x3, matrix products: 78 us -> 125 us  [project(): lax.dot_general(coeffs, vectors_now, (((0,), (0,)), ((), ())), precision=...]
where the time goes in v1:
time: 785 us; the launch traced here: 774 us
  waiting for transfers between devices  456 us (58%)
  matrix products  239 us (30%)
  other arithmetic  51.9 us (7%)
  between operations  14.8 us (2%)
  local copies, waits for them, and re-layouts  11.7 us (1%)
    psum x2, waiting for transfers between devices, shards(): applied = lax.psum(partial_sum, 'rows')  210 us
    dot_general x3, matrix products, project(): lax.dot_general(coeffs, vectors_now, (((0,), (0,)), ((), ())), precision=...  125 us
    all_gather x3, waiting for transfers between devices, forward(): parts = lax.all_gather(x, 'aux')  109 us
    psum x2, waiting for transfers between devices, shards(): correlation = lax.psum(local_gram, 'aux')  83.1 us
    dot_general x2, matrix products, shards(): jnp.dot(pair_coeffs, scaled, precision=highest, preferred_element_type=jn...  69.5 us
    psum x1, waiting for transfers between devices, shards(): rayleigh = lax.psum(local_rayleigh, 'rows')  54.8 us
    another operation x6, other arithmetic, shards(): factor = jnp.linalg.cholesky(correlation)  24.8 us
    dot_general x2, matrix products, shards(): jnp.dot(applied.T, applied, precision=highest, preferred_element_type=jnp...  23.5 us
  transfers between devices with their start and end apart: 8, of which 8 were waited for; matrix products, arithmetic and copies ran while one was open for 0% of the time, Pallas kernels for 0%

profile of v1, /device:TPU:0, one launch (start us, length us, event | category | flops | bytes accessed | tf_op | source)
XLA Modules:
  0.0 774.5 jit_solution(10525577226178895978)
XLA Ops:
  7.2 73.7 %fusion.19 = f32[1024,128]{1,0:T(8,128)} fusion(f32[9000,1024]{1,0:T(8,128)} %param.6, f32[9000,128]{1,0:T(8,128)} %param.8), kind=kOutput, calls=%fused_computation.33 | convolution fusion | flops 14155776000 | bytes 41996288 | tf_op jit(solution)/shard_map/dot_general | solution.py:10
  81.0 38.0 %all-gather.7.cloned.1.call-done = f32[4096,128]{1,0:T(8,128)} async-done(((f32[1024,128]{1,0:T(8,128)}), f32[4096,128]{1,0:T(8,128)}) %all-gather.7.cloned.1.call-update) | async-done | bytes 2097168 | tf_op jit(solution)/shard_map/all_gather | solution.py:25
  120.8 34.8 %convolution_bitcast_fusion.1 = f32[9000,128]{1,0:T(8,128)} fusion(f32[9000,1024]{1,0:T(8,128)} %param.6, f32[1024,128]{1,0:T(8,128)S(1)} %reduce_sum.27, f32[1024]{0:T(1024)S(1)} %add_divide_fusion), kind=kOutput, calls=%fused_computation.1 | convolution fusion | flops 14155907072 | bytes 42000384 | tf_op jit(solution)/shard_map/dot_general | solution.py:33
  155.6 105.0 %all-reduce.6.cloned.1.call-done = f32[9000,128]{1,0:T(8,128)} async-done(((f32[9000,128]{1,0:T(8,128)}), f32[9000,128]{1,0:T(8,128)}) %all-reduce.6.cloned.1.call-update) | async-done | bytes 4608016 | tf_op jit(solution)/shard_map/psum | solution.py:36
  260.6 11.8 %fusion.20 = f32[128,128]{0,1:T(8,128)} fusion(f32[9000,128]{1,0:T(8,128)} %all-reduce.6.cloned.1.call-done), kind=kOutput, calls=%fused_computation.34 | convolution fusion | flops 1769472000 | bytes 4673536 | tf_op jit(solution)/shard_map/dot_general | solution.py:37
  272.7 41.5 %all-reduce.8.cloned.1.call-done = f32[128,128]{0,1:T(8,128)} async-done(((f32[128,128]{0,1:T(8,128)}), f32[128,128]{0,1:T(8,128)}) %all-reduce.8.cloned.1.call-update) | async-done | bytes 65552 | tf_op jit(solution)/shard_map/psum | solution.py:40
  316.0 11.7 %cholesky.44 = f32[128,128]{1,0:T(8,128)S(1)} custom-call(f32[128,128]{1,0:T(8,128)S(1)} %fusion.16), custom_call_target="Cholesky" | custom-call | tf_op jit(solution)/shard_map/jit(cholesky)/cholesky | solution.py:41
  329.1 9.8 %custom-call.6 = f32[1,128,128]{1,2,0:T(8,128)S(1)} custom-call(f32[1,128,128]{2,1,0:T(8,128)S(1)} %fusion.11), custom_call_target="InvertDiagBlocksLowerTriangular" | custom-call | tf_op jit(solution)/shard_map/jit(_solve_triangular)/triangular_solve | solution.py:42
  338.9 9.6 %fusion.2 = f32[128,9000]{0,1:T(8,128)S(1)} fusion(f32[9000,128]{1,0:T(8,128)} %all-reduce.6.cloned.1.call-done, f32[1,128,128]{1,2,0:T(8,128)S(1)} %custom-call.6), kind=kOutput, calls=%fused_computation.4 | convolution fusion | flops 1769472000 | bytes 9281536 | tf_op jit(solution)/shard_map/jit(_solve_triangular)/triangular_solve | solution.py:42
  348.5 25.7 %convolution_bitcast_fusion.3 = f32[1024,128]{0,1:T(8,128)} fusion(f32[128,9000]{0,1:T(8,128)S(1)} %fusion.2, f32[9000,1024]{1,0:T(8,128)} %param.6), kind=kOutput, calls=%fused_computation.7 | convolution fusion | flops 14155776000 | bytes 41996288 | tf_op jit(solution)/shard_map/dot_general | solution.py:10
  374.3 35.3 %all-gather.9.cloned.1.call-done = f32[4096,128]{0,1:T(8,128)} async-done(((f32[1024,128]{0,1:T(8,128)}), f32[4096,128]{0,1:T(8,128)}) %all-gather.9.cloned.1.call-update) | async-done | bytes 2097168 | tf_op jit(solution)/shard_map/all_gather | solution.py:25
  409.6 2.8 reshape.14
  414.0 34.8 %convolution_bitcast_fusion = f32[9000,128]{1,0:T(8,128)} fusion(f32[9000,1024]{1,0:T(8,128)} %param.6, f32[1024,128]{1,0:T(8,128)S(1)} %copy.15, f32[1024]{0:T(1024)S(1)} %add_divide_fusion), kind=kOutput, calls=%fused_computation | convolution fusion | flops 14155907072 | bytes 42000384 | tf_op jit(solution)/shard_map/dot_general | solution.py:33
  449.0 104.8 %all-reduce.10.cloned.1.call-done = f32[9000,128]{1,0:T(8,128)} async-done(((f32[9000,128]{1,0:T(8,128)}), f32[9000,128]{1,0:T(8,128)}) %all-reduce.10.cloned.1.call-update) | async-done | bytes 4608016 | tf_op jit(solution)/shard_map/psum | solution.py:36
  553.8 11.8 %fusion.21 = f32[128,128]{0,1:T(8,128)} fusion(f32[9000,128]{1,0:T(8,128)} %all-reduce.10.cloned.1.call-done), kind=kOutput, calls=%fused_computation.35 | convolution fusion | flops 1769472000 | bytes 4673536 | tf_op jit(solution)/shard_map/dot_general | solution.py:37
  565.9 41.5 %all-reduce.12.cloned.1.call-done = f32[128,128]{0,1:T(8,128)} async-done(((f32[128,128]{0,1:T(8,128)}), f32[128,128]{0,1:T(8,128)}) %all-reduce.12.cloned.1.call-update) | async-done | bytes 65552 | tf_op jit(solution)/shard_map/psum | solution.py:40
  609.2 11.7 %cholesky.55 = f32[128,128]{1,0:T(8,128)S(1)} custom-call(f32[128,128]{1,0:T(8,128)S(1)} %fusion.14), custom_call_target="Cholesky" | custom-call | tf_op jit(solution)/shard_map/jit(cholesky)/cholesky | solution.py:41
  622.2 9.8 %custom-call.7 = f32[1,128,128]{1,2,0:T(8,128)S(1)} custom-call(f32[1,128,128]{2,1,0:T(8,128)S(1)} %fusion.12), custom_call_target="InvertDiagBlocksLowerTriangular" | custom-call | tf_op jit(solution)/shard_map/jit(_solve_triangular)/triangular_solve | solution.py:42
  632.0 9.5 %fusion = f32[128,9000]{0,1:T(8,128)S(1)} fusion(f32[9000,128]{1,0:T(8,128)} %all-reduce.10.cloned.1.call-done, f32[1,128,128]{1,2,0:T(8,128)S(1)} %custom-call.7), kind=kOutput, calls=%fused_computation.2 | convolution fusion | flops 1769472000 | bytes 9281536 | tf_op jit(solution)/shard_map/jit(_solve_triangular)/triangular_solve | solution.py:42
  641.6 2.1 copy-done
  643.7 25.7 %convolution_bitcast_fusion.2 = f32[1024,128]{0,1:T(8,128)} fusion(f32[128,9000]{0,1:T(8,128)S(1)} %fusion, f32[9000,1024]{1,0:T(8,128)} %param.6), kind=kOutput, calls=%fused_computation.6 | convolution fusion | flops 14155776000 | bytes 41996288 | tf_op jit(solution)/shard_map/dot_general | solution.py:10
  669.5 35.3 %all-gather.11.cloned.1.call-done = f32[4096,128]{0,1:T(8,128)} async-done(((f32[1024,128]{0,1:T(8,128)}), f32[4096,128]{0,1:T(8,128)}) %all-gather.11.cloned.1.call-update) | async-done | bytes 2097168 | tf_op jit(solution)/shard_map/all_gather | solution.py:25
  704.8 3.0 reshape.15
  710.7 54.8 %all-reduce.14.cloned.1.call-done = f32[128,128]{1,0:T(8,128)} async-done(((f32[128,128]{1,0:T(8,128)}), f32[128,128]{1,0:T(8,128)}) %all-reduce.14.cloned.1.call-update) | async-done | bytes 65552 | tf_op jit(solution)/shard_map/psum | solution.py:50
  (37 shorter events, 15.1 us)
Async XLA Ops:
  7.2 73.8 %copy-start.1 = (f32[1024]{0:T(1024)S(1)}, f32[1024]{0:T(1024)}, u32[]{:S(2)}) copy-start(f32[1024]{0:T(1024)} %param.7) | copy-start | bytes 12292
  7.2 111.8 %all-gather.7.cloned.1.call-start = ((), (), s32[]{:S(2)}) async-start(), calls=%async_computation.5 | async-start | bytes 2621440 | tf_op jit(solution)/shard_map/all_gather | solution.py:25
  81.0 179.7 %all-reduce.6.cloned.1.call-start = ((), (), s32[]{:S(2)}) async-start(), calls=%async_computation | async-start | bytes 9216000 | tf_op jit(solution)/shard_map/psum | solution.py:36
  155.6 158.6 %all-reduce.8.cloned.1.call-start = ((), (), s32[]{:S(2)}) async-start(), calls=%async_computation.1 | async-start | bytes 131072 | tf_op jit(solution)/shard_map/psum | solution.py:40
  272.4 137.2 %all-gather.9.cloned.1.call-start = ((), (), s32[]{:S(2)}) async-start(), calls=%async_computation.6 | async-start | bytes 2621440 | tf_op jit(solution)/shard_map/all_gather | solution.py:25
  374.3 179.5 %all-reduce.10.cloned.1.call-start = ((), (), s32[]{:S(2)}) async-start(), calls=%async_computation.2 | async-start | bytes 9216000 | tf_op jit(solution)/shard_map/psum | solution.py:36
  448.7 158.6 %all-reduce.12.cloned.1.call-start = ((), (), s32[]{:S(2)}) async-start(), calls=%async_computation.3 | async-start | bytes 131072 | tf_op jit(solution)/shard_map/psum | solution.py:40
  565.6 139.2 %all-gather.11.cloned.1.call-start = ((), (), s32[]{:S(2)}) async-start(), calls=%async_computation.7 | async-start | bytes 2621440 | tf_op jit(solution)/shard_map/all_gather | solution.py:25
  641.6 2.2 copy-start
  669.5 96.1 %all-reduce.14.cloned.1.call-start = ((), (), s32[]{:S(2)}) async-start(), calls=%async_computation.4 | async-start | bytes 131072 | tf_op jit(solution)/shard_map/psum | solution.py:50
Sparse Core Ops, SparseCore 0:
  81.1 37.8 all-gather.6
  155.7 104.8 all-reduce.5
  272.5 41.6 all-reduce.7
  374.4 35.1 all-gather.8
  448.9 104.8 all-reduce.9
  565.7 41.6 all-reduce.11
  669.6 35.1 all-gather.10
  710.9 54.6 all-reduce.13
